TPU v7x, 32 devices: a whole 2x2x4 slice. The times are simulated.
32 devices in a mesh: dp: 8 (over y, x, core), mp: 4 (over z).
Axes of the slice: x: 2, y: 2, z: 4, core: 2. Of those that a mesh axis runs over, the one named last changes fastest.
Arguments:
- hidden: bfloat16 [4096, 16384], P('dp', 'mp'), may hold values from -64 to 64
- key_weight: bfloat16 [16384, 1024], P(('mp', 'dp')), may hold values from -0.046875 to 0.046875
- key_state: float32 [16384], P(('mp', 'dp')), may hold values from 2.9802323e-09 to 1.1920929e-07
- key_cotangent: bfloat16 [4096, 1024], P('dp'), may hold values from -6 to 6
- doc_lengths: int32 [16, 4], P('dp'), may hold values from 1 to 128, 256 in all within a row
Outputs:
- input_grad: bfloat16 [4096, 16384], P('dp', 'mp')
- new_weight: bfloat16 [16384, 1024], P(('mp', 'dp'))
- new_state: float32 [16384], P(('mp', 'dp'))
Inputs may be any that keep to these rules, and one draw needn't show every extreme that they name: `doc_lengths`: each row lists the lengths of the documents of one sequence, in order, summing to 256.
All inputs are finite; a program needn't handle non-finite values.
Results may differ from a plain program's by a relative error of at most 0.0045.
Values may be sent and summed in bfloat16 or wider, within the bound.
A program may use at most 128 MiB of HBM per device.

v0:
```python
import jax
import jax.numpy as jnp
from jax import lax
from jax.sharding import PartitionSpec as P

HD = 128
LEN = 256


learn_rate = 0.01


def positions_of(doc_lengths):
    doc_ends = jnp.cumsum(doc_lengths, axis=1)
    doc_starts = doc_ends - doc_lengths
    places = jnp.arange(LEN, dtype=jnp.int32)
    before = doc_starts[:, None, :] <= places[None, :, None]
    doc_start = jnp.max(jnp.where(before, doc_starts[:, None, :], 0), axis=2)
    return (places[None, :] - doc_start).reshape(-1)


def rope_back(cotangent, positions):
    half_dim = HD // 2
    frequency = jnp.exp(
        -(2.0 * jnp.arange(half_dim, dtype=jnp.float32) / HD) * jnp.log(jnp.float32(500000.0))
    )
    angles = positions.astype(jnp.float32)[:, None] * frequency[None, :]
    cos_part = jnp.cos(angles)[:, None, :]
    sin_part = jnp.sin(angles)[:, None, :]
    gradients = cotangent.astype(jnp.float32).reshape(cotangent.shape[0], -1, HD)
    first_half = gradients[..., :half_dim]
    second_half = gradients[..., half_dim:]
    rotated = jnp.concatenate(
        [
            first_half * cos_part + second_half * sin_part,
            second_half * cos_part - first_half * sin_part,
        ],
        axis=-1,
    )
    return rotated.reshape(cotangent.shape[0], -1).astype(jnp.bfloat16)


def shards(hidden, key_weight, key_state, key_cotangent, doc_lengths):
    positions = positions_of(doc_lengths)
    key_grad = rope_back(key_cotangent, positions)
    gathered = lax.dot_general(
        key_grad,
        lax.all_gather(key_weight, "dp", axis=0, tiled=True),
        (((1,), (1,)), ((), ())),
        preferred_element_type=jnp.float32,
    )
    input_grad = gathered.astype(jnp.bfloat16)
    owned = lax.psum_scatter(
        lax.dot_general(
            hidden, key_grad, (((0,), (0,)), ((), ())), preferred_element_type=jnp.float32
        ),
        "dp",
        scatter_dimension=0,
        tiled=True,
    )
    squared = owned * owned
    squares_sum = lax.psum(jnp.sum(squared), ("dp", "mp"))
    clip_factor = jnp.minimum(jnp.float32(1.0), 1.0 / jnp.sqrt(squares_sum + 1e-06))
    row_mean = jnp.mean(squared, axis=1)
    new_state = key_state + clip_factor * clip_factor * row_mean
    step_size = learn_rate * clip_factor * owned / (jnp.sqrt(new_state)[:, None] + 1e-10)
    new_weight = (key_weight.astype(jnp.float32) - step_size).astype(jnp.bfloat16)
    new_weight, new_state = (new_weight, new_state)
    return (input_grad, new_weight, new_state)


def solution(mesh):
    return jax.shard_map(
        shards,
        mesh=mesh,
        in_specs=(
            P("dp", "mp"),
            P(("mp", "dp"), None),
            P(("mp", "dp")),
            P("dp", None),
            P("dp", None),
        ),
        out_specs=(P("dp", "mp"), P(("mp", "dp"), None), P(("mp", "dp"))),
        check_vma=False,
    )
```

profile of v0, /device:TPU:0, one launch (start us, length us, event | category | flops | bytes accessed | tf_op | source)
XLA Modules:
  0.0 240.6 jit_solution(537685099923209184)
XLA Ops:
  7.2 0.0 all-gather.2.cloned.1.call-start
  7.2 0.7 all-gather.2.cloned.1.call-update
  7.9 0.0 reduce-scatter.2.cloned.1.call-start
  7.9 0.9 reduce_window_sum.11
  8.8 0.7 sub.24
  9.5 0.1 select_reduce_fusion
  9.6 1.5 convert_bitcast_fusion
  11.1 0.5 copy.12
  11.5 1.0 multiply_cosine_fusion
  12.5 0.0 copy-start.2
  12.6 0.8 add_convert_fusion
  13.3 0.6 pad_maximum_fusion
  13.9 0.8 copy-done.2
  14.7 8.8 %convolution_bitcast_fusion = f32[4096,1024]{0,1:T(8,128)} fusion(bf16[512,4096]{1,0:T(8,128)(2,1)S(1)} %copy-done.2, bf16[64,8,8,128]{3,2,1,0:T(8,128)(2,1)S(1)} %bitcast.17), kind=kOutput, calls=%fused_computation | convolution fusion | flops 4294967296 | bytes 22020096 | tf_op jit(solution)/shard_map/dot_general | solution.py:54
  23.5 0.0 copy-start.1
  23.5 0.0 reduce-scatter.2.cloned.1.call-update
  23.5 1.2 copy-done.1
  24.7 0.5 copy.10
  25.3 41.6 %all-gather.2.cloned.1.call-done = bf16[4096,1024]{1,0:T(8,128)(2,1)} async-done(((bf16[512,1024]{1,0:T(8,128)(2,1)}), bf16[4096,1024]{1,0:T(8,128)(2,1)}) %all-gather.2.cloned.1.call-update) | async-done | bytes 8388624 | tf_op jit(solution)/shard_map/all_gather | solution.py:48
  66.9 9.5 %convolution_convert_fusion = bf16[512,4096]{1,0:T(8,128)(2,1)} fusion(bf16[4096,1024]{1,0:T(8,128)(2,1)} %all-gather.2.cloned.1.call-done, bf16[64,8,8,128]{3,2,1,0:T(8,128)(2,1)S(1)} %bitcast.18), kind=kOutput, calls=%fused_computation.1 | convolution fusion | flops 4297064448 | bytes 13631488 | tf_op jit(solution)/shard_map/dot_general | solution.py:46
  76.3 0.0 copy-start.3
  76.3 110.1 %reduce-scatter.2.cloned.1.call-done = f32[512,1024]{0,1:T(8,128)} async-done(((f32[4096,1024]{0,1:T(8,128)}), f32[512,1024]{0,1:T(8,128)}) %reduce-scatter.2.cloned.1.call-update) | async-done | bytes 2097168 | tf_op jit(solution)/shard_map/reduce_scatter | solution.py:53
  186.5 0.0 copy-start
  186.5 2.9 %multiply_reduce_fusion.1 = (f32[]{:T(128)}, f32[512]{0:T(512)S(1)}) fusion(f32[512,1024]{0,1:T(8,128)} %reduce-scatter.2.cloned.1.call-done), kind=kLoop, calls=%fused_computation.7 | loop fusion | flops 1572351 | bytes 2099204 | tf_op jit(solution)/shard_map/reduce_sum | solution.py:62
  189.4 39.5 %psum.7 = f32[]{:T(128)} all-reduce(f32[]{:T(128)} %get-tuple-element.9), channel_id=1, replica_groups=mesh['dp'=8,'mp'=4] {'dp','mp'}, use_global_device_ids=true, to_apply=%region_4.5 | all-reduce | flops 1 | bytes 8 | tf_op jit(solution)/shard_map/psum | solution.py:62
  229.5 0.0 copy-done.3
  229.5 0.6 sqrt_add_fusion
  230.1 0.0 copy-done
  230.1 1.4 subtract_convert_fusion
  231.5 2.3 copy.11
  (3 shorter events, 0.0 us)
Async XLA Ops:
  7.2 59.7 %all-gather.2.cloned.1.call-start = ((), (), s32[]{:S(2)}) async-start(), calls=%async_computation.1 | async-start | bytes 9437184 | tf_op jit(solution)/shard_map/all_gather | solution.py:48
  7.9 178.6 %reduce-scatter.2.cloned.1.call-start = ((), (), s32[]{:S(2)}) async-start(), calls=%async_computation.2 | async-start | bytes 18874368 | tf_op jit(solution)/shard_map/reduce_scatter | solution.py:53
  12.5 2.2 copy-start.2
  23.5 1.2 copy-start.1
  76.3 153.2 %copy-start.3 = (f32[512]{0:T(512)S(1)}, f32[512]{0:T(512)}, u32[]{:S(2)}) copy-start(f32[512]{0:T(512)} %param.7) | copy-start | bytes 6148
  186.5 43.6 %copy-start = (f32[512,1024]{0,1:T(8,128)S(1)}, f32[512,1024]{0,1:T(8,128)}, u32[]{:S(2)}) copy-start(f32[512,1024]{0,1:T(8,128)} %reduce-scatter.2.cloned.1.call-done) | copy-start | bytes 6291460
Sparse Core Ops, SparseCore 0:
  9.9 56.9 all-gather.1
  70.4 116.0 reduce-scatter.1
where the time goes:
time: 241 us
  waiting for transfers between devices  152 us (63%)
  blocking collectives  39.5 us (16%)
  matrix products  18.3 us (8%)
  between operations  14.8 us (6%)
  other arithmetic  10.3 us (4%)
  local copies, waits for them, and re-layouts  5.29 us (2%)
    reduce_scatter x1, waiting for transfers between devices, shards(): lax.psum_scatter(lax.dot_general(hidden, key_grad, (((0,), (0,)), ((), ()...  110 us
    all_gather x1, waiting for transfers between devices, shards(): lax.all_gather(key_weight, 'dp', axis=0, tiled=True)  41.6 us
    psum x1, blocking collectives, shards(): squares_sum = lax.psum(jnp.sum(squared), ('dp', 'mp'))  39.5 us
    dot_general x1, matrix products, shards(): lax.dot_general(key_grad, lax.all_gather(key_weight, 'dp', axis=0, tiled=...  9.47 us
    dot_general x1, matrix products, shards(): lax.dot_general(hidden, key_grad, (((0,), (0,)), ((), ())), preferred_ele...  8.79 us
    unnamed x12, local copies, waits for them, and re-layouts  5.29 us
  transfers between devices with their start and end apart: 2, of which 2 were waited for; matrix products, arithmetic and copies ran while one was open for 10% of the time, Pallas kernels for 0%

commit v1 on v0

--- a/solution.py
+++ b/solution.py
@@ -1,6 +1,8 @@
 import jax
 import jax.numpy as jnp
 from jax import lax
+from jax.experimental import pallas as pl
+from jax.experimental.pallas import tpu as pltpu
 from jax.sharding import PartitionSpec as P
 
 HD = 128
@@ -40,6 +42,17 @@
     return rotated.reshape(cotangent.shape[0], -1).astype(jnp.bfloat16)
 
 
+def update(owned, key_weight, key_state):
+    squared = owned * owned
+    squares_sum = lax.psum(jnp.sum(squared), ("dp", "mp"))
+    clip_factor = jnp.minimum(jnp.float32(1.0), 1.0 / jnp.sqrt(squares_sum + 1e-06))
+    row_mean = jnp.mean(squared, axis=1)
+    new_state = key_state + clip_factor * clip_factor * row_mean
+    step_size = learn_rate * clip_factor * owned / (jnp.sqrt(new_state)[:, None] + 1e-10)
+    new_weight = (key_weight.astype(jnp.float32) - step_size).astype(jnp.bfloat16)
+    return new_weight, new_state
+
+
 def shards(hidden, key_weight, key_state, key_cotangent, doc_lengths):
     positions = positions_of(doc_lengths)
     key_grad = rope_back(key_cotangent, positions)
@@ -58,20 +71,203 @@
         scatter_dimension=0,
         tiled=True,
     )
-    squared = owned * owned
-    squares_sum = lax.psum(jnp.sum(squared), ("dp", "mp"))
-    clip_factor = jnp.minimum(jnp.float32(1.0), 1.0 / jnp.sqrt(squares_sum + 1e-06))
-    row_mean = jnp.mean(squared, axis=1)
-    new_state = key_state + clip_factor * clip_factor * row_mean
-    step_size = learn_rate * clip_factor * owned / (jnp.sqrt(new_state)[:, None] + 1e-10)
-    new_weight = (key_weight.astype(jnp.float32) - step_size).astype(jnp.bfloat16)
-    new_weight, new_state = (new_weight, new_state)
-    return (input_grad, new_weight, new_state)
+    return (input_grad, *update(owned, key_weight, key_state))
+
+
+KG, HID, OWN_SIB, OWN_X, OWN_Y, RS1_X, RS1_Y, RS2_X, RS2_Y, FWD_X, FWD_Y, SIB_X, SIB_Y, SIB_D = (
+    0, 1, 5, 6, 8, 10, 12, 14, 15, 16, 17, 18, 19, 20)
+COPIES = 21
+
+
+def exchange(kg, hid, w, ig, g, wall, kgs, hs, part, s1x, s1y, r1x, r1y, s2x, s2y, r2x, r2y, send, recv):
+    f32 = jnp.float32
+    rows = w.shape[0]
+    half = rows // 2
+    cols = kg.shape[1] // 2
+    d = lax.axis_index("dp")
+    core, xb, yb = lax.rem(d, 2), lax.rem(d // 2, 2), d // 4
+    sib = d + 1 - 2 * core
+    xn = d + 2 - 4 * xb
+    yn = d + 4 - 8 * yb
+    dg = xn + 4 - 8 * yb
+
+    def sibling_of(block):
+        return block + 1 - 2 * core
+
+    def remote(place, src, dst, to):
+        return pltpu.make_async_remote_copy(
+            src_ref=src,
+            dst_ref=dst,
+            send_sem=send.at[place],
+            recv_sem=recv.at[place],
+            device_id={"dp": to},
+            device_id_type=pl.DeviceIdType.MESH,
+        )
+
+    barrier = pltpu.get_barrier_semaphore()
+    for to in (sib, xn, yn):
+        pl.semaphore_signal(barrier, inc=1, device_id={"dp": to}, device_id_type=pl.DeviceIdType.MESH)
+    pl.semaphore_wait(barrier, 3)
+
+    def columns(block, at=0, size=None):
+        size = rows if size is None else size
+        return pl.ds(pl.multiple_of(block * rows + at, size), size)
+
+    copies = {}
+
+    def begin(place, src, dst, to):
+        copies[place] = remote(place, src, dst, to)
+        copies[place].start()
+
+    first, second = pl.ds(0, half), pl.ds(half, half)
+    begin(OWN_X, w.at[first], wall.at[d, first], xn)
+    begin(OWN_Y, w.at[first], wall.at[d, first], yn)
+    begin(KG, kg, kgs, sib)
+    blocks = (dg, xn, yn, d)
+    for i, block in enumerate(blocks):
+        begin(HID + i, hid.at[:, columns(sibling_of(block))], hs.at[i], sib)
+    begin(OWN_SIB, w, wall.at[d], sib)
+
+    def dot_t(a, b):
+        return lax.dot_general(a, b, (((0,), (0,)), ((), ())), preferred_element_type=f32)
+
+    for i, block in enumerate(blocks):
+
+        @pl.loop(0, 2)
+        def _(t, i=i, block=block):
+            part[i, pl.ds(t * half, half), :] = dot_t(hid[:, columns(block, t * half, half)], kg[...])
+
+    copies[KG].wait_recv()
+    for i, block in enumerate(blocks):
+        copies[HID + i].wait_recv()
+
+        @pl.loop(0, 2)
+        def _(t, i=i):
+            at = pl.ds(t * half, half)
+            total = part[i, at, :] + dot_t(hs[i, :, pl.ds(pl.multiple_of(t * half, half), half)], kgs[...])
+            if i == 0:
+                s1x[0, at, :] = total[:, :cols].astype(jnp.bfloat16)
+                s1y[0, at, :] = total[:, cols:].astype(jnp.bfloat16)
+            else:
+                part[i, at, :] = total
+            if i == 1:
+                s1x[1, at, :] = total[:, :cols].astype(jnp.bfloat16)
+            if i == 2:
+                s1y[1, at, :] = total[:, cols:].astype(jnp.bfloat16)
+
+        if i == 0:
+            begin(RS1_X, s1x.at[0], r1x.at[0], xn)
+            begin(RS1_Y, s1y.at[0], r1y.at[0], yn)
+        if i == 1:
+            begin(RS1_X + 1, s1x.at[1], r1x.at[1], xn)
+        if i == 2:
+            begin(RS1_Y + 1, s1y.at[1], r1y.at[1], yn)
+    begin(OWN_X + 1, w.at[second], wall.at[d, second], xn)
+    begin(OWN_Y + 1, w.at[second], wall.at[d, second], yn)
+
+    def multiply(weights, block):
+        @pl.loop(0, 2)
+        def _(t):
+            ig[:, columns(block, t * half, half)] = lax.dot_general(
+                kg[...], weights[pl.ds(t * half, half), :], (((1,), (1,)), ((), ())), preferred_element_type=f32
+            ).astype(jnp.bfloat16)
+
+    multiply(w, d)
+    copies[OWN_SIB].wait_recv()
+    multiply(wall.at[sib], sib)
+
+    copies[RS1_X].wait_recv()
+
+    @pl.loop(0, 2)
+    def _(t):
+        at = pl.ds(t * half, half)
+        s2y[at, :] = (part[2, at, :cols] + r1x[0, at, :].astype(f32)).astype(jnp.bfloat16)
+
+    begin(RS2_Y, s2y, r2y, yn)
+    copies[RS1_Y].wait_recv()
+
+    @pl.loop(0, 2)
+    def _(t):
+        at = pl.ds(t * half, half)
+        s2x[at, :] = (part[1, at, cols:] + r1y[0, at, :].astype(f32)).astype(jnp.bfloat16)
+
+    begin(RS2_X, s2x, r2x, xn)
+    copies[OWN_X].wait_recv()
+    begin(FWD_Y, wall.at[xn, first], wall.at[xn, first], yn)
+    copies[OWN_Y + 1].wait_recv()
+    begin(FWD_X, wall.at[yn, second], wall.at[yn, second], xn)
+    copies[OWN_X + 1].wait_recv()
+    begin(SIB_X, wall.at[xn], wall.at[xn], sib)
+    copies[OWN_Y].wait_recv()
+    begin(SIB_Y, wall.at[yn], wall.at[yn], sib)
+    multiply(wall.at[xn], xn)
+    multiply(wall.at[yn], yn)
+    copies[SIB_X].wait_recv()
+    multiply(wall.at[sibling_of(xn)], sibling_of(xn))
+    copies[SIB_Y].wait_recv()
+    multiply(wall.at[sibling_of(yn)], sibling_of(yn))
+    copies[RS1_X + 1].wait_recv()
+    copies[RS1_Y + 1].wait_recv()
+    copies[RS2_X].wait_recv()
+    copies[RS2_Y].wait_recv()
+
+    @pl.loop(0, 2)
+    def _(t):
+        at = pl.ds(t * half, half)
+        g[at, :cols] = part[3, at, :cols] + r1x[1, at, :].astype(f32) + r2y[at, :].astype(f32)
+        g[at, cols:] = part[3, at, cols:] + r1y[1, at, :].astype(f32) + r2x[at, :].astype(f32)
+
+    copies[FWD_X].wait_recv()
+    copies[FWD_Y].wait_recv()
+    begin(SIB_D, wall.at[dg], wall.at[dg], sib)
+    multiply(wall.at[dg], dg)
+    copies[SIB_D].wait_recv()
+    multiply(wall.at[sibling_of(dg)], sibling_of(dg))
+    for copy in copies.values():
+        copy.wait_send()
+
+
+def shards_cube(hidden, key_weight, key_state, key_cotangent, doc_lengths):
+    key_grad = rope_back(key_cotangent, positions_of(doc_lengths))
+    tokens, width = hidden.shape
+    rows, kvw = key_weight.shape
+    cols = kvw // 2
+    bf16, f32 = jnp.bfloat16, jnp.float32
+    vmem = pl.BlockSpec(memory_space=pltpu.VMEM)
+    input_grad, owned = pl.pallas_call(
+        exchange,
+        out_shape=(
+            jax.ShapeDtypeStruct((tokens, width), bf16),
+            jax.ShapeDtypeStruct((rows, kvw), f32),
+        ),
+        in_specs=[vmem] * 3,
+        out_specs=(vmem, vmem),
+        scratch_shapes=[
+            pltpu.VMEM((width // rows, rows, kvw), bf16),
+            pltpu.VMEM((tokens, kvw), bf16),
+            pltpu.VMEM((4, tokens, rows), bf16),
+            pltpu.VMEM((4, rows, kvw), f32),
+            pltpu.VMEM((2, rows, cols), bf16),
+            pltpu.VMEM((2, rows, cols), bf16),
+            pltpu.VMEM((2, rows, cols), bf16),
+            pltpu.VMEM((2, rows, cols), bf16),
+            pltpu.VMEM((rows, cols), bf16),
+            pltpu.VMEM((rows, cols), bf16),
+            pltpu.VMEM((rows, cols), bf16),
+            pltpu.VMEM((rows, cols), bf16),
+            pltpu.SemaphoreType.DMA((COPIES,)),
+            pltpu.SemaphoreType.DMA((COPIES,)),
+        ],
+        compiler_params=pltpu.CompilerParams(
+            collective_id=0, has_side_effects=True, vmem_limit_bytes=58 * 1024 * 1024
+        ),
+    )(key_grad, hidden, key_weight)
+    return (input_grad, *update(owned, key_weight, key_state))
 
 
 def solution(mesh):
     return jax.shard_map(
-        shards,
+        shards_cube if mesh.shape["dp"] == 2**3 else shards,
         mesh=mesh,
         in_specs=(
             P("dp", "mp"),

time: 241 us -> 138 us (0.57)
  waiting for transfers between devices: 152 us -> 0 us
  Pallas kernels: 0 us -> 80.5 us
  matrix products: 18.3 us -> 0 us
  between operations: 14.8 us -> 1.4 us
    reduce_scatter x1 -> x0, waiting for transfers between devices: 110 us -> none  [shards(): lax.psum_scatter(lax.dot_general(hidden, key_grad, (((0,), (0,)), ((), ()...]
    pallas_call x0 -> x1, Pallas kernels: none -> 80.5 us  [shards_cube(): pl.pallas_call(exchange, out_shape=(jax.ShapeDtypeStruct((tokens, width),...]
    all_gather x1 -> x0, waiting for transfers between devices: 41.6 us -> none  [shards(): lax.all_gather(key_weight, 'dp', axis=0, tiled=True)]
    dot_general x2 -> x0, matrix products: 18.3 us -> none  [the longest x1 9.47 us: shards(): lax.dot_general(key_grad, lax.all_gather(key_weight, 'dp', axis=0, tiled=...]
  transfers between devices with their start and end apart: 2 -> 0, of which waited for: 2 -> 0; matrix products, arithmetic and copies ran while one was open for 10% -> 0% of each run, Pallas kernels for 0% -> 0%
where the time goes in v1:
time: 138 us; the launch traced here: 137 us
  Pallas kernels  80.5 us (58%)
  blocking collectives  40 us (29%)
  other arithmetic  10.5 us (8%)
  local copies, waits for them, and re-layouts  4.81 us (3%)
  between operations  1.4 us (1%)
    pallas_call x1, Pallas kernels, shards_cube(): pl.pallas_call(exchange, out_shape=(jax.ShapeDtypeStruct((tokens, width),...  80.5 us
    psum x1, blocking collectives, update(): squares_sum = lax.psum(jnp.sum(squared), ('dp', 'mp'))  40 us
    unnamed x12, local copies, waits for them, and re-layouts  4.81 us
    reduce_sum x1, other arithmetic, update(): squares_sum = lax.psum(jnp.sum(squared), ('dp', 'mp'))  2.92 us

profile of v1, /device:TPU:0, one launch (start us, length us, event | category | flops | bytes accessed | tf_op | source)
XLA Modules:
  0.0 137.2 jit_solution(11497673695612921578)
XLA Ops:
  0.6 0.9 reduce_window_sum.11
  1.5 0.7 sub.24
  2.2 0.1 select_reduce_fusion
  2.3 1.0 multiply_cosine_fusion
  3.3 1.5 %convert_bitcast_fusion = f32[64,8,8,128]{3,1,2,0:T(8,128)S(1)} fusion(bf16[512,1024]{1,0:T(8,128)(2,1)} %param.8), kind=kLoop, calls=%fused_computation | loop fusion | flops 524288 | bytes 3145728
  4.8 0.5 copy.8
  5.2 0.8 add_convert_fusion
  6.0 0.6 pad_maximum_fusion
  6.6 1.2 copy.12
  7.9 0.0 copy-start.2
  7.9 80.5 %shard_map.76 = (bf16[512,4096]{1,0:T(8,128)(2,1)}, f32[512,1024]{1,0:T(8,128)}) custom-call(bf16[512,1024]{1,0:T(8,128)(2,1)} %bitcast.12, bf16[512,4096]{1,0:T(8,128)(2,1)} %hid.1, bf16[512,1024]{1,0:T(8,128)(2,1)} %w.1), custom_call_target="tpu_custom_call" | custom-call | tf_op jit(solution)/shard_map/pallas_call | solution.py:237
  88.4 0.0 copy-start.3
  88.4 0.0 copy-start
  88.4 2.9 %multiply_reduce_fusion.1 = (f32[]{:T(128)}, f32[512]{0:T(512)S(1)}) fusion(f32[512,1024]{1,0:T(8,128)} %get-tuple-element.6), kind=kLoop, calls=%fused_computation.5 | loop fusion | flops 1572351 | bytes 2099204 | tf_op jit(solution)/shard_map/reduce_sum | solution.py:47
  91.3 40.0 %psum.7 = f32[]{:T(128)} all-reduce(f32[]{:T(128)} %get-tuple-element.7), channel_id=1, replica_groups=mesh['dp'=8,'mp'=4] {'dp','mp'}, use_global_device_ids=true, to_apply=%region_3.4 | all-reduce | flops 1 | bytes 8 | tf_op jit(solution)/shard_map/psum | solution.py:47
  132.0 0.0 copy-done.3
  132.0 0.6 sqrt_add_fusion
  132.6 0.0 copy-done.2
  132.6 0.0 copy-done
  132.6 0.0 copy-start.1
  132.6 1.5 %subtract_convert_fusion = bf16[512,1024]{1,0:T(8,128)(2,1)} fusion(f32[512,1024]{1,0:T(8,128)S(1)} %copy-done, bf16[512,1024]{1,0:T(8,128)(2,1)S(1)} %copy-done.2, f32[512]{0:T(512)S(1)} %get-tuple-element.9, f32[]{:T(128)S(6)} %mul_shard_map.3), kind=kLoop, calls=%fused_computation.1 | loop fusion | flops 2621440 | bytes 4196356 | tf_op jit(solution)/shard_map/convert_element_type | solution.py:52
  134.1 1.1 copy-done.1
  135.2 2.0 %copy.14 = bf16[512,4096]{1,0:T(8,128)(2,1)} copy(bf16[512,4096]{1,0:T(8,128)(2,1)S(1)} %copy-done.1) | data formatting | bytes 8388608
  (3 shorter events, 0.0 us)
Async XLA Ops:
  7.9 124.8 %copy-start.2 = (bf16[512,1024]{1,0:T(8,128)(2,1)S(1)}, bf16[512,1024]{1,0:T(8,128)(2,1)}, u32[]{:S(2)}) copy-start(bf16[512,1024]{1,0:T(8,128)(2,1)} %w.1) | copy-start | bytes 3145732
  88.4 43.6 %copy-start.3 = (f32[512]{0:T(512)S(1)}, f32[512]{0:T(512)}, u32[]{:S(2)}) copy-start(f32[512]{0:T(512)} %param.7) | copy-start | bytes 6148
  88.4 44.2 %copy-start = (f32[512,1024]{1,0:T(8,128)S(1)}, f32[512,1024]{1,0:T(8,128)}, u32[]{:S(2)}) copy-start(f32[512,1024]{1,0:T(8,128)} %get-tuple-element.6) | copy-start | bytes 6291460
  132.6 2.6 %copy-start.1 = (bf16[512,4096]{1,0:T(8,128)(2,1)S(1)}, bf16[512,4096]{1,0:T(8,128)(2,1)}, u32[]{:S(2)}) copy-start(bf16[512,4096]{1,0:T(8,128)(2,1)} %get-tuple-element.18) | copy-start | bytes 12582916

commit v2 on v1

--- a/solution.py
+++ b/solution.py
@@ -1,3 +1,5 @@
+import functools
+
 import jax
 import jax.numpy as jnp
 from jax import lax
@@ -79,7 +81,7 @@
 COPIES = 21
 
 
-def exchange(kg, hid, w, ig, g, wall, kgs, hs, part, s1x, s1y, r1x, r1y, s2x, s2y, r2x, r2y, send, recv):
+def exchange(zs, kg, hid, w, state, ig, new_w, new_state, g, squares, sums, got, wall, kgs, hs, part, s1x, s1y, r1x, r1y, s2x, s2y, r2x, r2y, send, recv, sum_send, sum_recv):
     f32 = jnp.float32
     rows = w.shape[0]
     half = rows // 2
@@ -105,9 +107,12 @@
         )
 
     barrier = pltpu.get_barrier_semaphore()
-    for to in (sib, xn, yn):
-        pl.semaphore_signal(barrier, inc=1, device_id={"dp": to}, device_id_type=pl.DeviceIdType.MESH)
-    pl.semaphore_wait(barrier, 3)
+    m = lax.axis_index("mp")
+    partners = [{"mp": m + bit - 2 * bit * lax.rem(m // bit, 2)} for bit in zs]
+    partners += [{"dp": sib}, {"dp": xn}, {"dp": yn}]
+    for to in partners:
+        pl.semaphore_signal(barrier, inc=1, device_id=to, device_id_type=pl.DeviceIdType.MESH)
+    pl.semaphore_wait(barrier, len(partners))
 
     def columns(block, at=0, size=None):
         size = rows if size is None else size
@@ -211,38 +216,89 @@
     copies[RS2_X].wait_recv()
     copies[RS2_Y].wait_recv()
 
-    @pl.loop(0, 2)
+    sums[0] = jnp.zeros_like(sums[0])
+
+    @pl.loop(0, 8)
     def _(t):
-        at = pl.ds(t * half, half)
-        g[at, :cols] = part[3, at, :cols] + r1x[1, at, :].astype(f32) + r2y[at, :].astype(f32)
-        g[at, cols:] = part[3, at, cols:] + r1y[1, at, :].astype(f32) + r2x[at, :].astype(f32)
-
+        at = pl.ds(pl.multiple_of(t * (rows // 8), rows // 8), rows // 8)
+        left = part[3, at, :cols] + r1x[1, at, :].astype(f32) + r2y[at, :].astype(f32)
+        right = part[3, at, cols:] + r1y[1, at, :].astype(f32) + r2x[at, :].astype(f32)
+        g[at, :cols] = left
+        g[at, cols:] = right
+        squared = left * left + right * right
+        squares[at, :] = jnp.sum(squared, axis=1, keepdims=True)
+        lanes = squared[:, :HD]
+        for k in range(1, cols // HD):
+            lanes += squared[:, k * HD : (k + 1) * HD]
+        sums[0] += jnp.sum(lanes.reshape(rows // 64, 8, HD), axis=0)
+
+    def sum_begin(stage):
+        copy = pltpu.make_async_remote_copy(
+            src_ref=sums.at[stage],
+            dst_ref=got.at[stage],
+            send_sem=sum_send.at[stage],
+            recv_sem=sum_recv.at[stage],
+            device_id=partners[stage],
+            device_id_type=pl.DeviceIdType.MESH,
+        )
+        copies["sum", stage] = copy
+        copy.start()
+
+    def sum_end(stage):
+        copies["sum", stage].wait_recv()
+        sums[stage + 1] = sums[stage] + got[stage]
+
+    last = len(partners) - 1
+    for stage in range(last - 1):
+        sum_begin(stage)
+        sum_end(stage)
+    sum_begin(last - 1)
     copies[FWD_X].wait_recv()
     copies[FWD_Y].wait_recv()
     begin(SIB_D, wall.at[dg], wall.at[dg], sib)
+    sum_end(last - 1)
+    sum_begin(last)
     multiply(wall.at[dg], dg)
     copies[SIB_D].wait_recv()
     multiply(wall.at[sibling_of(dg)], sibling_of(dg))
+    sum_end(last)
+    total = jnp.sum(jnp.sum(sums[last + 1], axis=0, keepdims=True), axis=1, keepdims=True)
+    clip = jnp.minimum(1.0, 1.0 / jnp.sqrt(total + 1e-06))
+
+    @pl.loop(0, 8)
+    def _(t):
+        at = pl.ds(pl.multiple_of(t * (rows // 8), rows // 8), rows // 8)
+        fresh = state[at, :] + clip * clip * (squares[at, :] / w.shape[1])
+        new_state[at, :] = fresh
+        scale = learn_rate * clip / (jnp.sqrt(fresh) + 1e-10)
+        new_w[at, :] = (w[at, :].astype(f32) - scale * g[at, :]).astype(jnp.bfloat16)
+
     for copy in copies.values():
         copy.wait_send()
 
 
-def shards_cube(hidden, key_weight, key_state, key_cotangent, doc_lengths):
+def shards_cube(zs, hidden, key_weight, key_state, key_cotangent, doc_lengths):
     key_grad = rope_back(key_cotangent, positions_of(doc_lengths))
     tokens, width = hidden.shape
     rows, kvw = key_weight.shape
     cols = kvw // 2
     bf16, f32 = jnp.bfloat16, jnp.float32
     vmem = pl.BlockSpec(memory_space=pltpu.VMEM)
-    input_grad, owned = pl.pallas_call(
-        exchange,
+    stages = len(zs) + 3
+    input_grad, new_weight, new_state = pl.pallas_call(
+        functools.partial(exchange, zs),
         out_shape=(
             jax.ShapeDtypeStruct((tokens, width), bf16),
-            jax.ShapeDtypeStruct((rows, kvw), f32),
+            jax.ShapeDtypeStruct((rows, kvw), bf16),
+            jax.ShapeDtypeStruct((rows, 1), f32),
         ),
-        in_specs=[vmem] * 3,
-        out_specs=(vmem, vmem),
+        in_specs=[vmem] * 4,
+        out_specs=(vmem, vmem, vmem),
         scratch_shapes=[
+            pltpu.VMEM((rows, kvw), f32),
+            pltpu.VMEM((rows, 1), f32),
+            pltpu.VMEM((stages + 1, 8, HD), f32),
+            pltpu.VMEM((stages, 8, HD), f32),
             pltpu.VMEM((width // rows, rows, kvw), bf16),
             pltpu.VMEM((tokens, kvw), bf16),
             pltpu.VMEM((4, tokens, rows), bf16),
@@ -257,17 +313,22 @@
             pltpu.VMEM((rows, cols), bf16),
             pltpu.SemaphoreType.DMA((COPIES,)),
             pltpu.SemaphoreType.DMA((COPIES,)),
+            pltpu.SemaphoreType.DMA((stages,)),
+            pltpu.SemaphoreType.DMA((stages,)),
         ],
         compiler_params=pltpu.CompilerParams(
             collective_id=0, has_side_effects=True, vmem_limit_bytes=58 * 1024 * 1024
         ),
-    )(key_grad, hidden, key_weight)
-    return (input_grad, *update(owned, key_weight, key_state))
+    )(key_grad, hidden, key_weight, key_state[:, None])
+    return input_grad, new_weight, new_state[:, 0]
 
 
 def solution(mesh):
+    mp = mesh.shape["mp"]
+    zs = tuple(2**k for k in range(mp.bit_length() - 1))
+    cube = mesh.shape["dp"] == 2**3 and mp == 2 ** len(zs)
     return jax.shard_map(
-        shards_cube if mesh.shape["dp"] == 2**3 else shards,
+        functools.partial(shards_cube, zs) if cube else shards,
         mesh=mesh,
         in_specs=(
             P("dp", "mp"),

time: 138 us -> 100 us (0.72)
  blocking collectives: 40 us -> 0 us
  local copies, waits for them, and re-layouts: 4.81 us -> 9.02 us
  other arithmetic: 10.5 us -> 7.14 us
  Pallas kernels: 80.5 us -> 83.3 us
    psum x1 -> x0, blocking collectives: 40 us -> none  [update(): squares_sum = lax.psum(jnp.sum(squared), ('dp', 'mp'))]
    reduce_sum x1 -> x0, other arithmetic: 2.92 us -> none  [update(): squares_sum = lax.psum(jnp.sum(squared), ('dp', 'mp'))]
    pallas_call x1, Pallas kernels: 80.5 us -> 83.3 us  [shards_cube(): pl.pallas_call(functools.partial(exchange, zs), out_shape=(jax.ShapeDtype...]
    unnamed x12 -> x7, local copies, waits for them, and re-layouts: 4.81 us -> 7.48 us
    pallas_call x0 -> x1, other arithmetic: none -> 1.68 us  [shards_cube(): pl.pallas_call(functools.partial(exchange, zs), out_shape=(jax.ShapeDtype...]
    broadcast_in_dim x0 -> x1, local copies, waits for them, and re-layouts: none -> 1.54 us  [shards_cube(): key_state[:, None]]
    convert_element_type x1 -> x0, other arithmetic: 1.5 us -> none  [update(): (key_weight.astype(jnp.float32) - step_size).astype(jnp.bfloat16)]
where the time goes in v2:
time: 100 us
  Pallas kernels  83.3 us (83%)
  local copies, waits for them, and re-layouts  9.02 us (9%)
  other arithmetic  7.14 us (7%)
    pallas_call x1, Pallas kernels, shards_cube(): pl.pallas_call(functools.partial(exchange, zs), out_shape=(jax.ShapeDtype...  83.3 us
    unnamed x7, local copies, waits for them, and re-layouts  7.48 us

profile of v2, /device:TPU:0, one launch (start us, length us, event | category | flops | bytes accessed | tf_op | source)
XLA Modules:
  0.0 100.1 jit_solution(14040533197243685061)
XLA Ops:
  0.6 0.9 reduce_window_sum.11
  1.5 0.7 sub.21
  2.2 0.1 select_reduce_fusion
  2.3 1.5 %copy.9.state = f32[512,1]{1,0:T(8,128)} copy(f32[512,1]{0,1:T(1,128)} %bitcast.15) | data formatting | bytes 4096 | tf_op jit(solution)/shard_map/broadcast_in_dim | solution.py:322
  3.8 1.0 multiply_cosine_fusion
  4.8 1.5 %convert_bitcast_fusion = f32[64,8,8,128]{3,1,2,0:T(8,128)S(1)} fusion(bf16[512,1024]{1,0:T(8,128)(2,1)} %param.8), kind=kLoop, calls=%fused_computation | loop fusion | flops 524288 | bytes 3145728
  6.3 0.5 copy.10
  6.8 0.8 add_convert_fusion
  7.6 0.6 pad_maximum_fusion
  8.1 1.2 %copy.14 = bf16[64,8,8,128]{3,1,2,0:T(8,128)(2,1)} copy(bf16[64,8,8,128]{3,2,1,0:T(8,128)(2,1)S(1)} %bitcast.13) | data formatting | bytes 2097152
  9.4 83.3 %shard_map.76 = (bf16[512,4096]{1,0:T(8,128)(2,1)}, bf16[512,1024]{1,0:T(8,128)(2,1)}, f32[512,1]{1,0:T(8,128)}) custom-call(bf16[512,1024]{1,0:T(8,128)(2,1)} %bitcast.12, bf16[512,4096]{1,0:T(8,128)(2,1)} %hid.1, bf16[512,1024]{1,0:T(8,128)(2,1)} %w.1, f32[512,1]{1,0:T(8,128)} %copy.9.state), custom_call_target="tpu_custom_call" | custom-call | tf_op jit(solution)/shard_map/pallas_call | solution.py:288
  92.7 1.7 %reduce = f32[512]{0:T(512)} reduce(f32[512,1]{1,0:T(8,128)} %get-tuple-element.8, f32[]{:T(128)} %constant.15), dimensions={1}, to_apply=%get-tuple-element.8.reduce_sub_computation | reduce | bytes 4100 | tf_op jit(solution)/shard_map/pallas_call | solution.py:288
  94.4 0.0 copy-start
  94.4 4.8 %copy.17 = bf16[512,4096]{1,0:T(8,128)(2,1)} copy(bf16[512,4096]{1,0:T(8,128)(2,1)} %get-tuple-element.16) | data formatting | bytes 8388608
  99.2 0.0 copy-done
  99.2 1.0 copy.18
  (3 shorter events, 0.0 us)
Async XLA Ops:
  94.4 4.8 %copy-start = (bf16[512,1024]{1,0:T(8,128)(2,1)S(1)}, bf16[512,1024]{1,0:T(8,128)(2,1)}, u32[]{:S(2)}) copy-start(bf16[512,1024]{1,0:T(8,128)(2,1)} %get-tuple-element.17) | copy-start | bytes 3145732
